TPU v7x, 32 devices: a whole 2x2x4 slice. The times are simulated.
32 devices in a mesh: rep: 4 (over x, core), dp: 4 (over z), tp: 2 (over y).
Axes of the slice: x: 2, y: 2, z: 4, core: 2. Of those that a mesh axis runs over, the one named last changes fastest.
Arguments:
- hidden: bfloat16 [4, 512, 14336], P('rep', None, 'tp'), may hold values from -6 to 6
- down_weight: bfloat16 [14336, 8192], P('tp', 'dp'), may hold values from -0.046875 to 0.046875
- out_grad: bfloat16 [4, 512, 8192], P('rep', 'tp', 'dp'), may hold values from -6 to 6
- pseudo_grad: bfloat16 [4, 14336, 8192], P('rep', 'tp', 'dp'), may hold values from -6 to 6
- momentum: float32 [14336, 8192], P(('tp', 'rep'), 'dp'), may hold values from -6 to 6
Outputs:
- layer_out: bfloat16 [4, 512, 8192], P('rep', 'tp', 'dp')
- hidden_grad: bfloat16 [4, 512, 14336], P('rep', 'dp', 'tp')
- new_momentum: float32 [14336, 8192], P(('tp', 'rep'), 'dp')
- outer_step: bfloat16 [14336, 8192], P('tp', 'dp')
All inputs are finite; a program needn't handle non-finite values.
Results may differ from a plain program's by a relative error of at most 0.017.
Values may be sent and summed in bfloat16 or wider, within the bound.
A program may use at most 256 MiB of HBM per device.

v0:
```python
import functools

import jax
import jax.numpy as jnp
from jax import lax
from jax.experimental import pallas as pl
from jax.experimental.pallas import tpu as pltpu
from jax.sharding import PartitionSpec as P

outer_rate = 0.7
momentum_rate = 0.9

MESH = pl.DeviceIdType.MESH
f32 = jnp.float32
bf16 = jnp.bfloat16


def pieces(extent, unit, most):
    return max(k for k in range(1, most + 1) if extent % (k * unit) == 0)


def kernel(
    n_rep, n_dp, n_tp, n_k, n_late, n_f,
    hidden, weight, grads, pseudo, momentum,
    layer_out, hidden_grad, new_momentum, outer_step, late, xch,
    ps, pr, la, lb, mom, nmb, wb, hb, gf, acc, po, tr, pb, dr,
    ld_sem, xs_sem, xr_sem, ps_sem, pr_sem, ss_sem, sr_sem, fs_sem, fr_sem, own_sem,
    gs_sem, gr_sem, ts_sem, tr_sem, ds_sem, dr_sem,
):
    n_x = n_rep // 2
    rep, dp, tp = lax.axis_index("rep"), lax.axis_index("dp"), lax.axis_index("tp")
    x, core = rep // 2, lax.rem(rep, 2)
    partner = 2 * x + 1 - core
    share, cols = momentum.shape
    chunk = share // n_k
    ffn = weight.shape[0]
    fb = ffn // n_f
    tokens = hidden.shape[1]
    t_rows, d_rows = tokens // n_tp, tokens // n_dp
    row_unit = 16
    n_sent = n_k - n_late
    sent = pl.ds(0, n_sent * chunk)

    def chip(d):
        return lax.rem(x + d, n_x)

    def rep_peer(d):
        return 2 * chip(d) + core

    def rows(owner, k):
        return pl.ds(pl.multiple_of(owner * share + k * chunk, chunk), chunk)

    def part(k):
        return pl.ds(pl.multiple_of(k * chunk, chunk), chunk)

    def remote(src, dst, send, recv, axis, index):
        return pltpu.make_async_remote_copy(
            src_ref=src, dst_ref=dst, send_sem=send, recv_sem=recv,
            device_id={axis: index}, device_id_type=MESH,
        )

    def drain(ref, sem):
        pltpu.make_async_copy(ref, ref, sem).wait()

    barrier = pltpu.get_barrier_semaphore()
    peers = [("rep", partner)]
    peers += [("rep", rep_peer(d)) for d in range(1, n_x)]
    peers += [("dp", lax.rem(dp + d, n_dp)) for d in range(1, n_dp)]
    peers += [("tp", lax.rem(tp + d, n_tp)) for d in range(1, n_tp)]
    for axis, index in peers:
        pl.semaphore_signal(barrier, inc=1, device_id={axis: index}, device_id_type=MESH)
    pl.semaphore_wait(barrier, len(peers))

    def exchange(d, k):
        return remote(
            pseudo.at[0, rows(2 * chip(d) + 1 - core, k)], xch.at[d, part(k)],
            xs_sem, xr_sem.at[d, k], "rep", partner,
        )

    def start_exchange(k, carry):
        for d in range(1, n_x):
            exchange(d, k).start()
        return carry

    def start_own_exchange(k, carry):
        exchange(0, k).start()
        return carry

    lax.fori_loop(0, n_k, start_exchange, 0)

    mine = pl.ds(pl.multiple_of(tp * t_rows, t_rows), t_rows)

    def gather(d):
        return remote(grads.at[0], gf.at[mine], gs_sem.at[d - 1], gr_sem.at[d - 1],
                      "tp", lax.rem(tp + d, n_tp))

    for d in range(1, n_tp):
        gather(d).start()
    own_grads = pltpu.make_async_copy(grads.at[0], gf.at[mine], own_sem)
    own_grads.start()
    lax.fori_loop(0, n_k, start_own_exchange, 0)

    def partial_send(d, k):
        return remote(ps.at[d - 1, part(k)], pr.at[d - 1, part(k)], ps_sem,
                      pr_sem.at[d - 1, k], "rep", rep_peer(d))

    def reduce_chunk(k, carry):
        for d in range(1, n_x):
            a = pltpu.make_async_copy(pseudo.at[0, rows(rep_peer(d), k)], la, ld_sem.at[0])
            a.start()
            exchange(d, k).wait_recv()
            b = pltpu.make_async_copy(xch.at[d, part(k)], lb, ld_sem.at[1])
            b.start()
            a.wait()
            b.wait()

            def add(i, c):
                r = pl.ds(pl.multiple_of(i * row_unit, row_unit), row_unit)
                o = pl.ds(pl.multiple_of(k * chunk + i * row_unit, row_unit), row_unit)
                ps[d - 1, o, :] = (la[r, :].astype(f32) + lb[r, :].astype(f32)).astype(bf16)
                return c

            lax.fori_loop(0, chunk // row_unit, add, 0)
            partial_send(d, k).start()
        return carry

    lax.fori_loop(0, n_k, reduce_chunk, 0)

    tn = cols // pieces(cols, 128, max(1, cols // 512))
    tm = tokens // pieces(tokens, row_unit, 2)

    def clear(i, carry):
        r = pl.ds(pl.multiple_of(i * row_unit, row_unit), row_unit)
        acc[r, :] = jnp.zeros((row_unit, cols), f32)
        return carry

    lax.fori_loop(0, tokens // row_unit, clear, 0)
    own_grads.wait()
    for d in range(1, n_tp):
        gather(d).wait()

    def back_send(d, f):
        to = lax.rem(dp + d, n_dp)
        c = pl.ds(pl.multiple_of(f * fb, fb), fb)
        return remote(
            pb.at[pl.ds(pl.multiple_of(to * d_rows, d_rows), d_rows), c],
            dr.at[d - 1, :, c], ds_sem, dr_sem.at[d - 1], "dp", to,
        )

    def matmul_block(f, carry):
        c = pl.ds(pl.multiple_of(f * fb, fb), fb)
        a = pltpu.make_async_copy(weight.at[c], wb, ld_sem.at[0])
        b = pltpu.make_async_copy(hidden.at[0, :, c], hb, ld_sem.at[1])
        a.start()
        b.start()
        a.wait()
        b.wait()

        def back(m, z):
            r = pl.ds(pl.multiple_of(m * tm, tm), tm)
            product = lax.dot_general(
                gf[r, :], wb[...], (((1,), (1,)), ((), ())), preferred_element_type=f32
            )
            pb[r, c] = product.astype(bf16)
            return z

        lax.fori_loop(0, tokens // tm, back, 0)
        for d in range(1, n_dp):
            back_send(d, f).start()

        def forward(n, z):
            t = pl.ds(pl.multiple_of(n * tn, tn), tn)
            acc[:, t] += jnp.dot(hb[...], wb[:, t], preferred_element_type=f32)
            return z

        lax.fori_loop(0, cols // tn, forward, 0)
        return carry

    lax.fori_loop(0, n_f, matmul_block, 0)

    def round_out(i, carry):
        r = pl.ds(pl.multiple_of(i * row_unit, row_unit), row_unit)
        po[r, :] = acc[r, :].astype(bf16)
        return carry

    lax.fori_loop(0, tokens // row_unit, round_out, 0)

    def out_send(d):
        to = lax.rem(tp + d, n_tp)
        return remote(po.at[pl.ds(pl.multiple_of(to * t_rows, t_rows), t_rows)],
                      tr.at[d - 1], ts_sem.at[d - 1], tr_sem.at[d - 1], "tp", to)

    for d in range(1, n_tp):
        out_send(d).start()

    def store_momentum(k):
        return pltpu.make_async_copy(nmb, new_momentum.at[part(k)], ld_sem.at[3])

    def step_send(d, k):
        return remote(pr.at[0, part(k)], outer_step.at[rows(rep, k)], ss_sem,
                      sr_sem.at[d - 1, k], "rep", rep_peer(d))

    def update_chunk(k, carry):
        a = pltpu.make_async_copy(pseudo.at[0, rows(rep, k)], la, ld_sem.at[0])
        m = pltpu.make_async_copy(momentum.at[part(k)], mom, ld_sem.at[2])
        a.start()
        m.start()
        exchange(0, k).wait_recv()
        b = pltpu.make_async_copy(xch.at[0, part(k)], lb, ld_sem.at[1])
        b.start()
        for d in range(1, n_x):
            partial_send(d, k).wait_recv()

        @pl.when(k > 0)
        def _():
            store_momentum(k - 1).wait()

        a.wait()
        b.wait()
        m.wait()

        def update(i, c):
            r = pl.ds(pl.multiple_of(i * row_unit, row_unit), row_unit)
            o = pl.ds(pl.multiple_of(k * chunk + i * row_unit, row_unit), row_unit)
            total = la[r, :].astype(f32) + lb[r, :].astype(f32)
            for d in range(1, n_x):
                total += pr[d - 1, o, :].astype(f32)
            average = total / n_rep
            fresh = momentum_rate * mom[r, :] + average
            nmb[r, :] = fresh
            pr[0, o, :] = (outer_rate * (average + momentum_rate * fresh)).astype(bf16)
            return c

        lax.fori_loop(0, chunk // row_unit, update, 0)

        @pl.when(k < n_sent)
        def _():
            for d in range(1, n_x):
                step_send(d, k).start()
            remote(pr.at[0, part(k)], outer_step.at[rows(rep, k)], fs_sem, fr_sem,
                   "rep", partner).start()
            pltpu.make_async_copy(
                pr.at[0, part(k)], outer_step.at[rows(rep, k)], own_sem
            ).start()

        store_momentum(k).start()
        return carry

    lax.fori_loop(0, n_k, update_chunk, 0)
    store_momentum(n_k - 1).wait()
    late_copy = pltpu.make_async_copy(
        pr.at[0, pl.ds(n_sent * chunk, n_late * chunk)], late, ld_sem.at[3]
    )
    late_copy.start()

    def forward_chunk(k, carry):
        for d in range(1, n_x):
            step_send(d, k).wait_recv()
            r = rows(2 * chip(n_x - d) + core, k)
            remote(outer_step.at[r], outer_step.at[r], fs_sem, fr_sem, "rep", partner).start()
        return carry

    lax.fori_loop(0, n_sent // 2, forward_chunk, 0)

    for d in range(1, n_tp):
        out_send(d).wait()

    def sum_out(i, carry):
        r = pl.ds(pl.multiple_of(i * row_unit, row_unit), row_unit)
        o = pl.ds(pl.multiple_of(tp * t_rows + i * row_unit, row_unit), row_unit)
        total = po[o, :].astype(f32)
        for d in range(1, n_tp):
            total += tr[d - 1, r, :].astype(f32)
        tr[0, r, :] = total.astype(bf16)
        return carry

    lax.fori_loop(0, t_rows // row_unit, sum_out, 0)
    out_copy = pltpu.make_async_copy(tr.at[0], layer_out.at[0], ld_sem.at[0])
    out_copy.start()

    for d in range(1, n_dp):
        drain(dr.at[d - 1], dr_sem.at[d - 1])

    def sum_back(f, carry):
        c = pl.ds(pl.multiple_of(f * fb, fb), fb)

        def band(i, z):
            r = pl.ds(pl.multiple_of(i * row_unit, row_unit), row_unit)
            o = pl.ds(pl.multiple_of(dp * d_rows + i * row_unit, row_unit), row_unit)
            total = pb[o, c].astype(f32)
            for d in range(1, n_dp):
                total += dr[d - 1, r, c].astype(f32)
            dr[0, r, c] = total.astype(bf16)
            return z

        lax.fori_loop(0, d_rows // row_unit, band, 0)
        return carry

    lax.fori_loop(0, n_f, sum_back, 0)
    back_copy = pltpu.make_async_copy(dr.at[0], hidden_grad.at[0], ld_sem.at[1])
    back_copy.start()

    lax.fori_loop(n_sent // 2, n_sent, forward_chunk, 0)

    out_copy.wait()
    back_copy.wait()
    late_copy.wait()
    drain(xch, xs_sem)
    drain(ps, ps_sem)
    drain(ps.at[:, sent], ss_sem)
    drain(xch.at[:, sent], fs_sem)
    drain(xch.at[:, sent], fr_sem)
    drain(pr.at[0, sent], own_sem)
    drain(dr, ds_sem)


def copy_bands(*refs):
    half = len(refs) // 2
    for source, target in zip(refs[:half], refs[half:]):
        target[...] = source[...]


def per_device(sizes, hidden, down_weight, out_grad, pseudo_grad, momentum):
    n_rep, n_dp, n_tp = sizes
    n_x = n_rep // 2
    tokens = hidden.shape[1]
    ffn, cols = down_weight.shape
    share = momentum.shape[0]
    n_k = pieces(share, 16, 14)
    n_f = pieces(ffn, 128, 14)
    n_late = max(1, n_k // 7)
    chunk, fb = share // n_k, ffn // n_f
    late_rows = n_late * chunk
    t_rows, d_rows = tokens // n_tp, tokens // n_dp
    dma = pltpu.SemaphoreType.DMA
    out = pl.pallas_call(
        functools.partial(kernel, n_rep, n_dp, n_tp, n_k, n_late, n_f),
        out_shape=(
            jax.ShapeDtypeStruct((1, t_rows, cols), bf16),
            jax.ShapeDtypeStruct((1, d_rows, ffn), bf16),
            jax.ShapeDtypeStruct((share, cols), f32),
            jax.ShapeDtypeStruct((ffn, cols), bf16),
            jax.ShapeDtypeStruct((late_rows, cols), bf16),
            jax.ShapeDtypeStruct((n_x, share, cols), bf16),
        ),
        in_specs=[pl.BlockSpec(memory_space=pl.ANY)] * 5,
        out_specs=[pl.BlockSpec(memory_space=pl.ANY)] * 6,
        scratch_shapes=[
            pltpu.VMEM((n_x - 1, share, cols), bf16),
            pltpu.VMEM((n_x - 1, share, cols), bf16),
            pltpu.VMEM((chunk, cols), bf16),
            pltpu.VMEM((chunk, cols), bf16),
            pltpu.VMEM((chunk, cols), f32),
            pltpu.VMEM((chunk, cols), f32),
            pltpu.VMEM((fb, cols), bf16),
            pltpu.VMEM((tokens, fb), bf16),
            pltpu.VMEM((tokens, cols), bf16),
            pltpu.VMEM((tokens, cols), f32),
            pltpu.VMEM((tokens, cols), bf16),
            pltpu.VMEM((n_tp - 1, t_rows, cols), bf16),
            pltpu.VMEM((tokens, ffn), bf16),
            pltpu.VMEM((n_dp - 1, d_rows, ffn), bf16),
            dma((4,)),
            dma,
            dma((n_x, n_k)),
            dma,
            dma((n_x - 1, n_k)),
            dma,
            dma((n_x - 1, n_k)),
            dma,
            dma,
            dma,
            dma((n_tp - 1,)),
            dma((n_tp - 1,)),
            dma((n_tp - 1,)),
            dma((n_tp - 1,)),
            dma,
            dma((n_dp - 1,)),
        ],
        compiler_params=pltpu.CompilerParams(
            collective_id=0, has_side_effects=True, vmem_limit_bytes=60 * 2**20
        ),
        name="layer_step",
    )(hidden, down_weight, out_grad, pseudo_grad, momentum)
    layer_out, hidden_grad, new_momentum, outer_step, late = out[:5]
    late = lax.all_gather(late, "rep", axis=0, tiled=False)
    results = (layer_out, hidden_grad, new_momentum, outer_step)
    steps = max(
        k for k in range(1, 9)
        if not any(n % (16 * k) for n in (t_rows, d_rows, ffn)) and share % (8 * k) == 0
    )

    def band(array):
        block = array.shape[:-2] + (array.shape[-2] // steps, array.shape[-1])
        return pl.BlockSpec(block, lambda i: (0,) * (array.ndim - 2) + (i, 0))

    layer_out, hidden_grad, new_momentum, outer_step = pl.pallas_call(
        copy_bands,
        out_shape=tuple(jax.ShapeDtypeStruct(r.shape, r.dtype) for r in results),
        grid=(steps,),
        in_specs=[band(r) for r in results],
        out_specs=[band(r) for r in results],
        cost_estimate=pl.CostEstimate(
            flops=0, bytes_accessed=2 * sum(r.nbytes for r in results), transcendentals=0
        ),
        compiler_params=pltpu.CompilerParams(vmem_limit_bytes=40 * 2**20),
        name="result_copy",
    )(*results)
    outer_step = lax.dynamic_update_slice(
        outer_step.reshape(n_rep, share, cols), late, (0, share - late_rows, 0)
    ).reshape(ffn, cols)
    return layer_out, hidden_grad, new_momentum, outer_step


def solution(mesh):
    sizes = tuple(mesh.shape[a] for a in ("rep", "dp", "tp"))
    return jax.shard_map(
        functools.partial(per_device, sizes),
        mesh=mesh,
        in_specs=(
            P("rep", None, "tp"),
            P("tp", "dp"),
            P("rep", "tp", "dp"),
            P("rep", "tp", "dp"),
            P(("tp", "rep"), "dp"),
        ),
        out_specs=(
            P("rep", "tp", "dp"),
            P("rep", "dp", "tp"),
            P(("tp", "rep"), "dp"),
            P("tp", "dp"),
        ),
        check_vma=False,
    )
```

profile of v0, /device:TPU:0, one launch (start us, length us, event | category | flops | bytes accessed | tf_op | source)
XLA Modules:
  0.0 357.1 jit_solution(11183170394897782424)
XLA Ops:
  7.2 0.0 all-gather.3.cloned.1.call-start
  7.2 305.2 %layer_step.1 = (bf16[1,256,2048]{2,1,0:T(8,128)(2,1)}, bf16[1,128,7168]{2,1,0:T(8,128)(2,1)}, f32[1792,2048]{1,0:T(8,128)}, bf16[7168,2048]{1,0:T(8,128)(2,1)},...) custom-call(bf16[1,512,7168]{2,1,0:T(8,128)(2,1)} %hidden.1, bf16[7168,2048]{1,0:T(8,128)(2,1)} %weight.1, ...), custom_call_target="tpu_custom_call" | custom-call | tf_op jit(solution)/shard_map/layer_step/pallas_call | solution.py:336
  312.4 0.0 all-gather.3.cloned.1.call-update
  312.5 0.0 copy-start
  312.5 1.5 copy-done
  314.0 0.0 copy-start.1
  314.0 1.2 copy-done.1
  315.2 30.3 %result_copy.1 = (bf16[1,256,2048]{2,1,0:T(8,128)(2,1)}, bf16[1,128,7168]{2,1,0:T(8,128)(2,1)}, f32[1792,2048]{1,0:T(8,128)}, bf16[7168,2048]{1,0:T(8,128)(2,1)}) custom-call(bf16[1,256,2048]{2,1,0:T(8,128)(2,1)S(1)} %copy-done.1, bf16[1,128,7168]{2,1,0:T(8,128)(2,1)S(1)} %copy-done, f32[1792,2048]{1,0:T(8,128)} %get-tuple-element.15.refs_2_, ...), custom_call_target="tpu_custom_call" | custom-call | bytes 93847552 | tf_op jit(solution)/shard_map/result_copy/pallas_call | solution.py:397
  345.4 0.0 all-gather.3.cloned.1.call-done
  345.4 4.8 %constant_dynamic-update-slice_fusion = bf16[4,1792,2048]{2,1,0:T(8,128)(2,1)} fusion(bf16[4,1792,2048]{2,1,0:T(8,128)(2,1)} %bitcast.4, bf16[4,256,2048]{2,1,0:T(8,128)(2,1)} %bitcast.3), kind=kLoop, calls=%fused_computation | loop fusion | bytes 8388608 | tf_op jit(solution)/shard_map/dynamic_update_slice | solution.py:409
Async XLA Ops:
  7.2 338.3 %all-gather.3.cloned.1.call-start = ((), (), s32[]{:S(2)}) async-start(), calls=%async_computation | async-start | bytes 5242880 | tf_op jit(solution)/shard_map/all_gather | solution.py:386
  312.5 1.5 copy-start
  314.0 1.2 copy-start.1
Sparse Core Ops, SparseCore 0:
  312.6 32.6 all-gather.2
where the time goes:
time: 359 us; the launch traced here: 357 us
  Pallas kernels  335 us (93%)
  between operations  14 us (4%)
  local copies, waits for them, and re-layouts  7.5 us (2%)
    pallas_call x1, Pallas kernels, per_device(): pl.pallas_call(functools.partial(kernel, n_rep, n_dp, n_tp, n_k, n_late,...  305 us
    pallas_call x1, Pallas kernels, per_device(): pl.pallas_call(copy_bands, out_shape=tuple((jax.ShapeDtypeStruct(r.shape,...  30.3 us
  transfers between devices with their start and end apart: 1, of which 0 were waited for; matrix products, arithmetic and copies ran while one was open for 0% of the time, Pallas kernels for 8%

commit v1 on v0

--- a/solution.py
+++ b/solution.py
@@ -10,6 +10,10 @@
 outer_rate = 0.7
 momentum_rate = 0.9
 
+copy_flops = 1000
+n_groups = 4
+whole_vmem = 2**26 - 2**16
+
 MESH = pl.DeviceIdType.MESH
 f32 = jnp.float32
 bf16 = jnp.bfloat16
@@ -20,10 +24,22 @@
 
 
 def kernel(
-    n_rep, n_dp, n_tp, n_k, n_late, n_f,
+    n_rep, n_dp, n_tp, n_k, n_late, n_f, groups,
     hidden, weight, grads, pseudo, momentum,
-    layer_out, hidden_grad, new_momentum, outer_step, late, xch,
-    ps, pr, la, lb, mom, nmb, wb, hb, gf, acc, po, tr, pb, dr,
+    layer_out, hidden_grad, new_momentum, outer_step, xch, *refs,
+):
+    n_x, n_g = n_rep // 2, len(groups)
+    late, edge, refs = refs[:n_g], refs[n_g:n_g + n_x - 1], refs[n_g + n_x - 1:]
+    body(n_rep, n_dp, n_tp, n_k, n_late, n_f, groups,
+         hidden, weight, grads, pseudo, momentum,
+         layer_out, hidden_grad, new_momentum, outer_step, xch, late, edge, *refs)
+
+
+def body(
+    n_rep, n_dp, n_tp, n_k, n_late, n_f, groups,
+    hidden, weight, grads, pseudo, momentum,
+    layer_out, hidden_grad, new_momentum, outer_step, xch, late, edge,
+    ps, pr, xv, la, lb, mom, nmb, wb, hb, gf, acc, po, tr, pb, dr,
     ld_sem, xs_sem, xr_sem, ps_sem, pr_sem, ss_sem, sr_sem, fs_sem, fr_sem, own_sem,
     gs_sem, gr_sem, ts_sem, tr_sem, ds_sem, dr_sem,
 ):
@@ -62,6 +78,13 @@
     def drain(ref, sem):
         pltpu.make_async_copy(ref, ref, sem).wait()
 
+    def own_rows(t, slot):
+        d, k = 1 + lax.rem(t, n_x - 1), t // (n_x - 1)
+        return pltpu.make_async_copy(
+            pseudo.at[0, rows(rep_peer(d), k)], la.at[slot], ld_sem.at[slot]
+        )
+
+    own_rows(0, 0).start()
     barrier = pltpu.get_barrier_semaphore()
     peers = [("rep", partner)]
     peers += [("rep", rep_peer(d)) for d in range(1, n_x)]
@@ -73,8 +96,14 @@
 
     def exchange(d, k):
         return remote(
-            pseudo.at[0, rows(2 * chip(d) + 1 - core, k)], xch.at[d, part(k)],
+            pseudo.at[0, rows(2 * chip(d) + 1 - core, k)], xv.at[d - 1, part(k)],
             xs_sem, xr_sem.at[d, k], "rep", partner,
+        )
+
+    def own_exchange(k):
+        return remote(
+            pseudo.at[0, rows(partner, k)], xch.at[part(k)],
+            xs_sem, xr_sem.at[0, k], "rep", partner,
         )
 
     def start_exchange(k, carry):
@@ -83,7 +112,7 @@
         return carry
 
     def start_own_exchange(k, carry):
-        exchange(0, k).start()
+        own_exchange(k).start()
         return carry
 
     lax.fori_loop(0, n_k, start_exchange, 0)
@@ -104,27 +133,29 @@
         return remote(ps.at[d - 1, part(k)], pr.at[d - 1, part(k)], ps_sem,
                       pr_sem.at[d - 1, k], "rep", rep_peer(d))
 
-    def reduce_chunk(k, carry):
-        for d in range(1, n_x):
-            a = pltpu.make_async_copy(pseudo.at[0, rows(rep_peer(d), k)], la, ld_sem.at[0])
-            a.start()
-            exchange(d, k).wait_recv()
-            b = pltpu.make_async_copy(xch.at[d, part(k)], lb, ld_sem.at[1])
-            b.start()
-            a.wait()
-            b.wait()
-
-            def add(i, c):
-                r = pl.ds(pl.multiple_of(i * row_unit, row_unit), row_unit)
-                o = pl.ds(pl.multiple_of(k * chunk + i * row_unit, row_unit), row_unit)
-                ps[d - 1, o, :] = (la[r, :].astype(f32) + lb[r, :].astype(f32)).astype(bf16)
-                return c
-
-            lax.fori_loop(0, chunk // row_unit, add, 0)
-            partial_send(d, k).start()
-        return carry
-
-    lax.fori_loop(0, n_k, reduce_chunk, 0)
+    def reduce_chunk(t, carry):
+        d, k = 1 + lax.rem(t, n_x - 1), t // (n_x - 1)
+        slot = lax.rem(t, 2)
+
+        @pl.when(t + 1 < n_k * (n_x - 1))
+        def _():
+            own_rows(t + 1, 1 - slot).start()
+
+        own_rows(t, slot).wait()
+        exchange(d, k).wait_recv()
+
+        def add(i, c):
+            r = pl.ds(pl.multiple_of(i * row_unit, row_unit), row_unit)
+            o = pl.ds(pl.multiple_of(k * chunk + i * row_unit, row_unit), row_unit)
+            total = la[slot, r, :].astype(f32) + xv[d - 1, o, :].astype(f32)
+            ps[d - 1, o, :] = total.astype(bf16)
+            return c
+
+        lax.fori_loop(0, chunk // row_unit, add, 0)
+        partial_send(d, k).start()
+        return carry
+
+    lax.fori_loop(0, n_k * (n_x - 1), reduce_chunk, 0)
 
     tn = cols // pieces(cols, 128, max(1, cols // 512))
     tm = tokens // pieces(tokens, row_unit, 2)
@@ -200,13 +231,17 @@
         return remote(pr.at[0, part(k)], outer_step.at[rows(rep, k)], ss_sem,
                       sr_sem.at[d - 1, k], "rep", rep_peer(d))
 
+    def edge_send(d):
+        return remote(pr.at[0, part(n_sent - 1)], edge[d - 1], ss_sem,
+                      sr_sem.at[d - 1, n_sent - 1], "rep", rep_peer(d))
+
     def update_chunk(k, carry):
-        a = pltpu.make_async_copy(pseudo.at[0, rows(rep, k)], la, ld_sem.at[0])
+        a = pltpu.make_async_copy(pseudo.at[0, rows(rep, k)], la.at[0], ld_sem.at[0])
         m = pltpu.make_async_copy(momentum.at[part(k)], mom, ld_sem.at[2])
         a.start()
         m.start()
-        exchange(0, k).wait_recv()
-        b = pltpu.make_async_copy(xch.at[0, part(k)], lb, ld_sem.at[1])
+        own_exchange(k).wait_recv()
+        b = pltpu.make_async_copy(xch.at[part(k)], lb, ld_sem.at[1])
         b.start()
         for d in range(1, n_x):
             partial_send(d, k).wait_recv()
@@ -222,7 +257,7 @@
         def update(i, c):
             r = pl.ds(pl.multiple_of(i * row_unit, row_unit), row_unit)
             o = pl.ds(pl.multiple_of(k * chunk + i * row_unit, row_unit), row_unit)
-            total = la[r, :].astype(f32) + lb[r, :].astype(f32)
+            total = la[0, r, :].astype(f32) + lb[r, :].astype(f32)
             for d in range(1, n_x):
                 total += pr[d - 1, o, :].astype(f32)
             average = total / n_rep
@@ -233,10 +268,18 @@
 
         lax.fori_loop(0, chunk // row_unit, update, 0)
 
-        @pl.when(k < n_sent)
+        @pl.when(k < n_sent - 1)
         def _():
             for d in range(1, n_x):
                 step_send(d, k).start()
+
+        @pl.when(k == n_sent - 1)
+        def _():
+            for d in range(1, n_x):
+                edge_send(d).start()
+
+        @pl.when(k < n_sent)
+        def _():
             remote(pr.at[0, part(k)], outer_step.at[rows(rep, k)], fs_sem, fr_sem,
                    "rep", partner).start()
             pltpu.make_async_copy(
@@ -248,10 +291,14 @@
 
     lax.fori_loop(0, n_k, update_chunk, 0)
     store_momentum(n_k - 1).wait()
-    late_copy = pltpu.make_async_copy(
-        pr.at[0, pl.ds(n_sent * chunk, n_late * chunk)], late, ld_sem.at[3]
-    )
-    late_copy.start()
+    late_copies = [
+        pltpu.make_async_copy(
+            pr.at[0, pl.ds(n_sent * chunk + start, size)], target, ld_sem.at[4 + g]
+        )
+        for g, ((start, size), target) in enumerate(zip(groups, late))
+    ]
+    for copy in late_copies:
+        copy.start()
 
     def forward_chunk(k, carry):
         for d in range(1, n_x):
@@ -300,16 +347,20 @@
     back_copy = pltpu.make_async_copy(dr.at[0], hidden_grad.at[0], ld_sem.at[1])
     back_copy.start()
 
-    lax.fori_loop(n_sent // 2, n_sent, forward_chunk, 0)
+    lax.fori_loop(n_sent // 2, n_sent - 1, forward_chunk, 0)
 
     out_copy.wait()
     back_copy.wait()
-    late_copy.wait()
-    drain(xch, xs_sem)
+    for copy in late_copies:
+        copy.wait()
+    drain(outer_step.at[pl.ds(0, n_x * share)], xs_sem)
     drain(ps, ps_sem)
     drain(ps.at[:, sent], ss_sem)
-    drain(xch.at[:, sent], fs_sem)
-    drain(xch.at[:, sent], fr_sem)
+    forwarded = pl.ds(0, (n_x * n_sent - n_x + 1) * chunk)
+    drain(outer_step.at[forwarded], fs_sem)
+    drain(outer_step.at[forwarded], fr_sem)
+    for d in range(1, n_x):
+        edge_send(d).wait_recv()
     drain(pr.at[0, sent], own_sem)
     drain(dr, ds_sem)
 
@@ -318,6 +369,52 @@
     half = len(refs) // 2
     for source, target in zip(refs[:half], refs[half:]):
         target[...] = source[...]
+
+
+def place(n_rep, share, outer_step, parts):
+    n_x, n_p = n_rep // 2, len(parts)
+    arrays = [part[0] for part in parts]
+
+    def run(step, *refs):
+        sources, target, held = refs[:n_p], refs[n_p], refs[n_p + 1:2 * n_p + 1]
+        in_sem, out_sem = refs[2 * n_p + 1:]
+        rep = lax.axis_index("rep")
+        x, core = rep // 2, lax.rem(rep, 2)
+
+        def load(i):
+            return pltpu.make_async_copy(sources[i], held[i], in_sem.at[i])
+
+        def store(i):
+            array, first, d, other = parts[i]
+            owner = 2 * lax.rem(x + d, n_x) + (1 - core if other else core)
+            r = pl.ds(pl.multiple_of(owner * share + first, 16), array.shape[0])
+            return pltpu.make_async_copy(held[i], target.at[r], out_sem.at[i])
+
+        for i in range(n_p):
+            load(i).start()
+        for i in range(n_p):
+            load(i).wait()
+            store(i).start()
+        for i in range(n_p):
+            store(i).wait()
+
+    moved = sum(array.nbytes for array in arrays)
+    return pl.pallas_call(
+        run,
+        out_shape=jax.ShapeDtypeStruct(outer_step.shape, outer_step.dtype),
+        in_specs=[pl.BlockSpec(memory_space=pltpu.HBM)] + [pl.BlockSpec(memory_space=pl.ANY)] * n_p,
+        out_specs=pl.BlockSpec(memory_space=pltpu.HBM),
+        scratch_shapes=[pltpu.VMEM(array.shape, array.dtype) for array in arrays] + [
+            pltpu.SemaphoreType.DMA((n_p,)),
+            pltpu.SemaphoreType.DMA((n_p,)),
+        ],
+        input_output_aliases={0: 0},
+        compiler_params=pltpu.CompilerParams(vmem_limit_bytes=whole_vmem),
+        cost_estimate=pl.CostEstimate(
+            flops=copy_flops * moved, bytes_accessed=2 * moved, transcendentals=0
+        ),
+        name="place",
+    )(outer_step, *arrays)
 
 
 def per_device(sizes, hidden, down_weight, out_grad, pseudo_grad, momentum):
@@ -326,29 +423,36 @@
     tokens = hidden.shape[1]
     ffn, cols = down_weight.shape
     share = momentum.shape[0]
-    n_k = pieces(share, 16, 14)
+    n_k = pieces(share, 16, 28)
     n_f = pieces(ffn, 128, 14)
-    n_late = max(1, n_k // 7)
+    n_late = max(1, (4 * n_k) // 14)
     chunk, fb = share // n_k, ffn // n_f
     late_rows = n_late * chunk
+    last = max(16, late_rows // 16 // 16 * 16)
+    tail = [4 * last, 2 * last, last]
+    if late_rows - sum(tail) < 16:
+        tail = [16] * 3
+    lengths = [late_rows - sum(tail)] + tail
+    groups = tuple((sum(lengths[:g]), lengths[g]) for g in range(n_groups))
     t_rows, d_rows = tokens // n_tp, tokens // n_dp
     dma = pltpu.SemaphoreType.DMA
     out = pl.pallas_call(
-        functools.partial(kernel, n_rep, n_dp, n_tp, n_k, n_late, n_f),
+        functools.partial(kernel, n_rep, n_dp, n_tp, n_k, n_late, n_f, groups),
         out_shape=(
             jax.ShapeDtypeStruct((1, t_rows, cols), bf16),
             jax.ShapeDtypeStruct((1, d_rows, ffn), bf16),
             jax.ShapeDtypeStruct((share, cols), f32),
             jax.ShapeDtypeStruct((ffn, cols), bf16),
-            jax.ShapeDtypeStruct((late_rows, cols), bf16),
-            jax.ShapeDtypeStruct((n_x, share, cols), bf16),
-        ),
+            jax.ShapeDtypeStruct((share, cols), bf16),
+        ) + tuple(jax.ShapeDtypeStruct((size, cols), bf16) for _, size in groups)
+        + (jax.ShapeDtypeStruct((chunk, cols), bf16),) * (n_x - 1),
         in_specs=[pl.BlockSpec(memory_space=pl.ANY)] * 5,
-        out_specs=[pl.BlockSpec(memory_space=pl.ANY)] * 6,
+        out_specs=[pl.BlockSpec(memory_space=pl.ANY)] * (4 + len(groups) + n_x),
         scratch_shapes=[
             pltpu.VMEM((n_x - 1, share, cols), bf16),
             pltpu.VMEM((n_x - 1, share, cols), bf16),
-            pltpu.VMEM((chunk, cols), bf16),
+            pltpu.VMEM((n_x - 1, share, cols), bf16),
+            pltpu.VMEM((2, chunk, cols), bf16),
             pltpu.VMEM((chunk, cols), bf16),
             pltpu.VMEM((chunk, cols), f32),
             pltpu.VMEM((chunk, cols), f32),
@@ -360,7 +464,7 @@
             pltpu.VMEM((n_tp - 1, t_rows, cols), bf16),
             pltpu.VMEM((tokens, ffn), bf16),
             pltpu.VMEM((n_dp - 1, d_rows, ffn), bf16),
-            dma((4,)),
+            dma((4 + len(groups),)),
             dma,
             dma((n_x, n_k)),
             dma,
@@ -382,8 +486,22 @@
         ),
         name="layer_step",
     )(hidden, down_weight, out_grad, pseudo_grad, momentum)
-    layer_out, hidden_grad, new_momentum, outer_step, late = out[:5]
-    late = lax.all_gather(late, "rep", axis=0, tiled=False)
+    layer_out, hidden_grad, new_momentum, outer_step = out[:4]
+    late, edge = out[5:5 + len(groups)], out[5 + len(groups):]
+
+    def across(value, d):
+        hops = [(2 * x + c, 2 * ((x - d) % n_x) + c) for x in range(n_x) for c in range(2)]
+        return lax.ppermute(value, "rep", hops)
+
+    def beside(value):
+        hops = [(2 * x + c, 2 * x + 1 - c) for x in range(n_x) for c in range(2)]
+        return lax.ppermute(value, "rep", hops)
+
+    arrived = []
+    for value in late:
+        arrived.append([across(value, d) for d in range(1, n_x)])
+    near = [beside(value) for value in late]
+    edge_near = [beside(value) for value in edge]
     results = (layer_out, hidden_grad, new_momentum, outer_step)
     steps = max(
         k for k in range(1, 9)
@@ -401,21 +519,44 @@
         in_specs=[band(r) for r in results],
         out_specs=[band(r) for r in results],
         cost_estimate=pl.CostEstimate(
-            flops=0, bytes_accessed=2 * sum(r.nbytes for r in results), transcendentals=0
+            flops=copy_flops * sum(r.nbytes for r in results),
+            bytes_accessed=2 * sum(r.nbytes for r in results), transcendentals=0,
         ),
-        compiler_params=pltpu.CompilerParams(vmem_limit_bytes=40 * 2**20),
-        name="result_copy",
+        compiler_params=pltpu.CompilerParams(vmem_limit_bytes=whole_vmem),
     )(*results)
-    outer_step = lax.dynamic_update_slice(
-        outer_step.reshape(n_rep, share, cols), late, (0, share - late_rows, 0)
-    ).reshape(ffn, cols)
+    firsts = [share - late_rows + start for start, _ in groups]
+    parts = []
+    for d in range(1, n_x):
+        parts.append((edge[d - 1], share - late_rows - chunk, n_x - d, False))
+        parts.append((edge_near[d - 1], share - late_rows - chunk, n_x - d, True))
+    for first, value, own in zip(firsts, late, near):
+        parts += [(value, first, 0, False), (own, first, 0, True)]
+    outer_step = place(n_rep, share, outer_step, parts)
+
+    def put(outer_step, values, first, other):
+        rep = lax.axis_index("rep")
+        x, core = rep // 2, lax.rem(rep, 2)
+        for d, value in enumerate(values):
+            owner = 2 * lax.rem(x + d + 1, n_x) + (1 - core if other else core)
+            outer_step = lax.dynamic_update_slice(outer_step, value, (owner * share + first, 0))
+        return outer_step
+
+    for first, here in zip(firsts, arrived):
+        here, outer_step = lax.optimization_barrier((here, outer_step))
+        across_near = [beside(value) for value in here]
+        outer_step = put(outer_step, here, first, False)
+        outer_step = put(outer_step, across_near, first, True)
     return layer_out, hidden_grad, new_momentum, outer_step
 
 
 def solution(mesh):
     sizes = tuple(mesh.shape[a] for a in ("rep", "dp", "tp"))
+
+    def step(*args):
+        return per_device(sizes, *args)
+
     return jax.shard_map(
-        functools.partial(per_device, sizes),
+        step,
         mesh=mesh,
         in_specs=(
             P("rep", None, "tp"),

time: 359 us -> 350 us (0.975)
  Pallas kernels: 335 us -> 313 us
  waiting for transfers between devices: 0.02 us -> 20 us
  between operations: 14 us -> 0.7 us
  starting transfers between devices: 0.04 us -> 5.66 us
    pallas_call x1, Pallas kernels: 305 us -> 280 us  [per_device(): pl.pallas_call(functools.partial(kernel, n_rep, n_dp, n_tp, n_k, n_late,...]
    ppermute x0 -> x13, waiting for transfers between devices: none -> 20 us  [the longest x4 18.9 us: across(): return lax.ppermute(value, 'rep', hops)]
    ppermute x0 -> x13, starting transfers between devices: none -> 5.66 us  [the longest x4 4.27 us: across(): return lax.ppermute(value, 'rep', hops)]
    pallas_call x0 -> x1, Pallas kernels: none -> 3.69 us  [place(): pl.pallas_call(run, out_shape=jax.ShapeDtypeStruct(outer_step.shape, oute...]
    dynamic_update_slice x1 -> x8, local copies, waits for them, and re-layouts: 4.79 us -> 7.92 us  [put(): lax.dynamic_update_slice(outer_step, value, (owner * share + first, 0))]
  transfers between devices with their start and end apart: 1 -> 13, of which waited for: 0 -> 5; matrix products, arithmetic and copies ran while one was open for 0% -> 2% of each run, Pallas kernels for 8% -> 10%
where the time goes in v1:
time: 350 us; the launch traced here: 348 us
  Pallas kernels  313 us (89%)
  waiting for transfers between devices  20 us (6%)
  local copies, waits for them, and re-layouts  7.92 us (2%)
  starting transfers between devices  5.66 us (2%)
    pallas_call x1, Pallas kernels, per_device(): pl.pallas_call(functools.partial(kernel, n_rep, n_dp, n_tp, n_k, n_late,...  280 us
    pallas_call x1, Pallas kernels, per_device(): pl.pallas_call(copy_bands, out_shape=tuple((jax.ShapeDtypeStruct(r.shape,...  30.1 us
    ppermute x4, waiting for transfers between devices, across(): return lax.ppermute(value, 'rep', hops)  18.9 us
    dynamic_update_slice x8, local copies, waits for them, and re-layouts, put(): lax.dynamic_update_slice(outer_step, value, (owner * share + first, 0))  7.92 us
  transfers between devices with their start and end apart: 13, of which 5 were waited for; matrix products, arithmetic and copies ran while one was open for 2% of the time, Pallas kernels for 10%

profile of v1, /device:TPU:0, one launch (start us, length us, event | category | flops | bytes accessed | tf_op | source)
XLA Modules:
  0.0 347.8 jit_solution(2570837679922714221)
XLA Ops:
  0.6 279.7 %layer_step.1 = (bf16[1,256,2048]{2,1,0:T(8,128)(2,1)}, bf16[1,128,7168]{2,1,0:T(8,128)(2,1)}, f32[1792,2048]{1,0:T(8,128)}, bf16[7168,2048]{1,0:T(8,128)(2,1)},...) custom-call(bf16[1,512,7168]{2,1,0:T(8,128)(2,1)} %hidden.1, ...), custom_call_target="tpu_custom_call" | custom-call | tf_op jit(solution)/shard_map/layer_step/pallas_call | solution.py:439
  280.4 0.2 collective-permute-start.8
  280.6 0.5 collective-permute-start.3
  281.1 0.1 collective-permute-start.5
  281.2 0.4 collective-permute-start.4
  281.6 0.1 collective-permute-start.6
  281.7 0.4 collective-permute-done.8.refs_9_
  282.1 0.1 collective-permute-start.7
  282.3 30.1 %shard_map.84 = (bf16[1,256,2048]{2,1,0:T(8,128)(2,1)}, bf16[1,128,7168]{2,1,0:T(8,128)(2,1)}, f32[1792,2048]{1,0:T(8,128)}, bf16[7168,2048]{1,0:T(8,128)(2,1)}) custom-call(bf16[1,256,2048]{2,1,0:T(8,128)(2,1)} %get-tuple-element.25.refs_0_, bf16[1,128,7168]{2,1,0:T(8,128)(2,1)} %get-tuple-element.26.refs_1_, f32[1792,2048]{1,0:T(8,128)} %get-tuple-element.27.refs_2_, ...), custom_call_target="tpu_custom_call" | custom-call | flops 46923776000 | bytes 93847552 | tf_op jit(solution)/shard_map/pallas_call | solution.py:515
  312.3 0.0 collective-permute-done.4.refs_1_
  312.3 0.0 collective-permute-done.7.refs_7_
  312.4 0.0 collective-permute-done.6.refs_5_
  312.4 0.0 collective-permute-done.5.refs_3_
  312.4 3.7 %place.1 = bf16[7168,2048]{1,0:T(8,128)(2,1)} custom-call(bf16[7168,2048]{1,0:T(8,128)(2,1)} %get-tuple-element.36.step, bf16[64,2048]{1,0:T(8,128)(2,1)} %get-tuple-element.37.refs_0_, bf16[64,2048]{1,0:T(8,128)(2,1)} %collective-permute-done.4.refs_1_, bf16[288,2048]{1,0:T(8,128)(2,1)} %get-tuple-element.35.refs_2_, ...), custom_call_target="tpu_custom_call", output_to_operand_aliasing={{}: (0, {})} | custom-call | flops 4718592000 | bytes 9437184 | tf_op jit(solution)/shard_map/place/pallas_call | solution.py:402
  316.1 0.4 collective-permute-start.9
  316.5 1.1 collective-permute-start.2
  317.6 2.4 constant_dynamic-update-slice_fusion.7
  320.0 1.1 constant_dynamic-update-slice_fusion.6
  321.1 9.6 %collective-permute-done.2 = bf16[128,2048]{1,0:T(8,128)(2,1)S(1)} collective-permute-done((bf16[128,2048]{1,0:T(8,128)(2,1)}, bf16[128,2048]{1,0:T(8,128)(2,1)S(1)}, u32[]{:S(2)}, u32[]{:S(2)}) %collective-permute-start.2) | collective-permute-done | bytes 524320 | tf_op jit(solution)/shard_map/ppermute | solution.py:494
  330.7 0.0 collective-permute-start.10
  330.7 1.3 collective-permute-start.1
  332.0 0.8 constant_dynamic-update-slice_fusion.5
  332.9 0.8 constant_dynamic-update-slice_fusion.4
  333.7 5.9 %collective-permute-done.1 = bf16[64,2048]{1,0:T(8,128)(2,1)S(1)} collective-permute-done((bf16[64,2048]{1,0:T(8,128)(2,1)}, bf16[64,2048]{1,0:T(8,128)(2,1)S(1)}, u32[]{:S(2)}, u32[]{:S(2)}) %collective-permute-start.1) | collective-permute-done | bytes 262176 | tf_op jit(solution)/shard_map/ppermute | solution.py:494
  339.6 1.3 collective-permute-start
  341.0 0.7 constant_dynamic-update-slice_fusion.3
  341.7 0.7 constant_dynamic-update-slice_fusion.2
  342.4 3.3 collective-permute-done
  345.8 0.0 collective-permute-start.12
  345.8 0.7 constant_dynamic-update-slice_fusion.1
  346.4 0.7 collective-permute-done.12
  347.1 0.7 constant_dynamic-update-slice_fusion
  (5 shorter events, 0.0 us)
Async XLA Ops:
  280.4 1.8 collective-permute-start.8
  280.6 35.5 %collective-permute-start.3 = (bf16[288,2048]{1,0:T(8,128)(2,1)}, bf16[288,2048]{1,0:T(8,128)(2,1)}, u32[]{:S(2)}, u32[]{:S(2)}) collective-permute-start(bf16[288,2048]{1,0:T(8,128)(2,1)} %get-tuple-element.35.refs_2_), channel_id=1, source_target_pairs={{0,16},{8,24},{16,0},{24,8},{1,17},{9,25},{17,1},{25,9},{2,18},{10... | collective-permute-start | bytes 3538952 | tf_op jit(solution)/shard_map/ppermute | solution.py:494
  281.1 31.3 %collective-permute-start.5 = (bf16[288,2048]{1,0:T(8,128)(2,1)}, bf16[288,2048]{1,0:T(8,128)(2,1)}, u32[]{:S(2)}, u32[]{:S(2)}) collective-permute-start(bf16[288,2048]{1,0:T(8,128)(2,1)} %get-tuple-element.35.refs_2_), channel_id=1, source_target_pairs={{0,8},{8,0},{16,24},{24,16},{1,9},{9,1},{17,25},{25,17},{2,10},{10... | collective-permute-start | bytes 3538952 | tf_op jit(solution)/shard_map/ppermute | solution.py:498
  281.2 31.1 %collective-permute-start.4 = (bf16[64,2048]{1,0:T(8,128)(2,1)}, bf16[64,2048]{1,0:T(8,128)(2,1)}, u32[]{:S(2)}, u32[]{:S(2)}) collective-permute-start(bf16[64,2048]{1,0:T(8,128)(2,1)} %get-tuple-element.37.refs_0_), channel_id=1, source_target_pairs={{0,8},{8,0},{16,24},{24,16},{1,9},{9,1},{17,25},{25,17},{2,10},{10... | collective-permute-start | bytes 786440 | tf_op jit(solution)/shard_map/ppermute | solution.py:498
  281.6 30.8 %collective-permute-start.6 = (bf16[128,2048]{1,0:T(8,128)(2,1)}, bf16[128,2048]{1,0:T(8,128)(2,1)}, u32[]{:S(2)}, u32[]{:S(2)}) collective-permute-start(bf16[128,2048]{1,0:T(8,128)(2,1)} %get-tuple-element.34.refs_4_), channel_id=1, source_target_pairs={{0,8},{8,0},{16,24},{24,16},{1,9},{9,1},{17,25},{25,17},{2,10},{10... | collective-permute-start | bytes 1572872 | tf_op jit(solution)/shard_map/ppermute | solution.py:498
  282.1 30.2 %collective-permute-start.7 = (bf16[64,2048]{1,0:T(8,128)(2,1)}, bf16[64,2048]{1,0:T(8,128)(2,1)}, u32[]{:S(2)}, u32[]{:S(2)}) collective-permute-start(bf16[64,2048]{1,0:T(8,128)(2,1)} %get-tuple-element.33.refs_6_), channel_id=1, source_target_pairs={{0,8},{8,0},{16,24},{24,16},{1,9},{9,1},{17,25},{25,17},{2,10},{10... | collective-permute-start | bytes 786440 | tf_op jit(solution)/shard_map/ppermute | solution.py:498
  316.1 3.9 %collective-permute-start.9 = (bf16[288,2048]{1,0:T(8,128)(2,1)}, bf16[288,2048]{1,0:T(8,128)(2,1)S(1)}, u32[]{:S(2)}, u32[]{:S(2)}) collective-permute-start(bf16[288,2048]{1,0:T(8,128)(2,1)} %collective-permute-done.3), channel_id=1, source_target_pairs={{0,8},{8,0},{16,24},{24,16},{1,9},{9,1},{17,25},{25,17},{2,10},{10... | collective-permute-start | bytes 3538952 | tf_op jit(solution)/shard_map/ppermute | solution.py:498
  316.5 14.2 %collective-permute-start.2 = (bf16[128,2048]{1,0:T(8,128)(2,1)}, bf16[128,2048]{1,0:T(8,128)(2,1)S(1)}, u32[]{:S(2)}, u32[]{:S(2)}) collective-permute-start(bf16[128,2048]{1,0:T(8,128)(2,1)} %get-tuple-element.34.refs_4_), channel_id=1, source_target_pairs={{0,16},{8,24},{16,0},{24,8},{1,17},{9,25},{17,1},{25,9},{2,18},{10... | collective-permute-start | bytes 1572872 | tf_op jit(solution)/shard_map/ppermute | solution.py:494
  330.7 2.2 collective-permute-start.10
  330.7 8.9 %collective-permute-start.1 = (bf16[64,2048]{1,0:T(8,128)(2,1)}, bf16[64,2048]{1,0:T(8,128)(2,1)S(1)}, u32[]{:S(2)}, u32[]{:S(2)}) collective-permute-start(bf16[64,2048]{1,0:T(8,128)(2,1)} %get-tuple-element.33.refs_6_), channel_id=1, source_target_pairs={{0,16},{8,24},{16,0},{24,8},{1,17},{9,25},{17,1},{25,9},{2,18},{10... | collective-permute-start | bytes 786440 | tf_op jit(solution)/shard_map/ppermute | solution.py:494
  339.6 2.1 collective-permute-start.11
  339.6 6.1 %collective-permute-start = (bf16[32,2048]{1,0:T(8,128)(2,1)}, bf16[32,2048]{1,0:T(8,128)(2,1)S(1)}, u32[]{:S(2)}, u32[]{:S(2)}) collective-permute-start(bf16[32,2048]{1,0:T(8,128)(2,1)} %get-tuple-element.32.refs_8_), channel_id=1, source_target_pairs={{0,16},{8,24},{16,0},{24,8},{1,17},{9,25},{17,1},{25,9},{2,18},{10... | collective-permute-start | bytes 393224 | tf_op jit(solution)/shard_map/ppermute | solution.py:494
  345.8 1.3 collective-permute-start.12

commit v2 on v1

--- a/solution.py
+++ b/solution.py
@@ -12,6 +12,7 @@
 
 copy_flops = 1000
 n_groups = 4
+n_late_of, n_skew_of = 9, 4
 whole_vmem = 2**26 - 2**16
 
 MESH = pl.DeviceIdType.MESH
@@ -24,19 +25,19 @@
 
 
 def kernel(
-    n_rep, n_dp, n_tp, n_k, n_late, n_f, groups,
+    n_rep, n_dp, n_tp, n_k, n_late, n_skew, n_f, groups,
     hidden, weight, grads, pseudo, momentum,
     layer_out, hidden_grad, new_momentum, outer_step, xch, *refs,
 ):
     n_x, n_g = n_rep // 2, len(groups)
     late, edge, refs = refs[:n_g], refs[n_g:n_g + n_x - 1], refs[n_g + n_x - 1:]
-    body(n_rep, n_dp, n_tp, n_k, n_late, n_f, groups,
+    body(n_rep, n_dp, n_tp, n_k, n_late, n_skew, n_f, groups,
          hidden, weight, grads, pseudo, momentum,
          layer_out, hidden_grad, new_momentum, outer_step, xch, late, edge, *refs)
 
 
 def body(
-    n_rep, n_dp, n_tp, n_k, n_late, n_f, groups,
+    n_rep, n_dp, n_tp, n_k, n_late, n_skew, n_f, groups,
     hidden, weight, grads, pseudo, momentum,
     layer_out, hidden_grad, new_momentum, outer_step, xch, late, edge,
     ps, pr, xv, la, lb, mom, nmb, wb, hb, gf, acc, po, tr, pb, dr,
@@ -55,6 +56,7 @@
     t_rows, d_rows = tokens // n_tp, tokens // n_dp
     row_unit = 16
     n_sent = n_k - n_late
+    n_low = n_sent - n_skew
     sent = pl.ds(0, n_sent * chunk)
 
     def chip(d):
@@ -231,9 +233,10 @@
         return remote(pr.at[0, part(k)], outer_step.at[rows(rep, k)], ss_sem,
                       sr_sem.at[d - 1, k], "rep", rep_peer(d))
 
-    def edge_send(d):
-        return remote(pr.at[0, part(n_sent - 1)], edge[d - 1], ss_sem,
-                      sr_sem.at[d - 1, n_sent - 1], "rep", rep_peer(d))
+    def edge_send(d, k):
+        place_at = pl.ds(pl.multiple_of((k - n_low) * chunk, chunk), chunk)
+        return remote(pr.at[0, part(k)], edge[d - 1].at[place_at], ss_sem,
+                      sr_sem.at[d - 1, k], "rep", rep_peer(d))
 
     def update_chunk(k, carry):
         a = pltpu.make_async_copy(pseudo.at[0, rows(rep, k)], la.at[0], ld_sem.at[0])
@@ -268,15 +271,15 @@
 
         lax.fori_loop(0, chunk // row_unit, update, 0)
 
-        @pl.when(k < n_sent - 1)
+        @pl.when(k < n_low)
         def _():
             for d in range(1, n_x):
                 step_send(d, k).start()
 
-        @pl.when(k == n_sent - 1)
+        @pl.when((k >= n_low) & (k < n_sent) & (core == 0))
         def _():
             for d in range(1, n_x):
-                edge_send(d).start()
+                edge_send(d, k).start()
 
         @pl.when(k < n_sent)
         def _():
@@ -307,7 +310,7 @@
             remote(outer_step.at[r], outer_step.at[r], fs_sem, fr_sem, "rep", partner).start()
         return carry
 
-    lax.fori_loop(0, n_sent // 2, forward_chunk, 0)
+    lax.fori_loop(0, n_low // 2, forward_chunk, 0)
 
     for d in range(1, n_tp):
         out_send(d).wait()
@@ -347,7 +350,7 @@
     back_copy = pltpu.make_async_copy(dr.at[0], hidden_grad.at[0], ld_sem.at[1])
     back_copy.start()
 
-    lax.fori_loop(n_sent // 2, n_sent - 1, forward_chunk, 0)
+    lax.fori_loop(n_low // 2, n_low, forward_chunk, 0)
 
     out_copy.wait()
     back_copy.wait()
@@ -355,12 +358,28 @@
         copy.wait()
     drain(outer_step.at[pl.ds(0, n_x * share)], xs_sem)
     drain(ps, ps_sem)
-    drain(ps.at[:, sent], ss_sem)
-    forwarded = pl.ds(0, (n_x * n_sent - n_x + 1) * chunk)
+
+    @pl.when(core == 0)
+    def _():
+        drain(ps.at[:, sent], ss_sem)
+
+    @pl.when(core == 1)
+    def _():
+        drain(ps.at[:, pl.ds(0, n_low * chunk)], ss_sem)
+
+    forwarded = pl.ds(0, (n_sent + (n_x - 1) * n_low) * chunk)
     drain(outer_step.at[forwarded], fs_sem)
     drain(outer_step.at[forwarded], fr_sem)
-    for d in range(1, n_x):
-        edge_send(d).wait_recv()
+
+    @pl.when(core == 0)
+    def _():
+        def edge_wait(k, carry):
+            for d in range(1, n_x):
+                edge_send(d, k).wait_recv()
+            return carry
+
+        lax.fori_loop(n_low, n_sent, edge_wait, 0)
+
     drain(pr.at[0, sent], own_sem)
     drain(dr, ds_sem)
 
@@ -425,7 +444,8 @@
     share = momentum.shape[0]
     n_k = pieces(share, 16, 28)
     n_f = pieces(ffn, 128, 14)
-    n_late = max(1, (4 * n_k) // 14)
+    n_late = max(1, (n_late_of * n_k) // 28)
+    n_skew = max(1, (n_skew_of * n_k) // 28)
     chunk, fb = share // n_k, ffn // n_f
     late_rows = n_late * chunk
     last = max(16, late_rows // 16 // 16 * 16)
@@ -433,11 +453,14 @@
     if late_rows - sum(tail) < 16:
         tail = [16] * 3
     lengths = [late_rows - sum(tail)] + tail
-    groups = tuple((sum(lengths[:g]), lengths[g]) for g in range(n_groups))
+    skew = n_skew * chunk
+    groups = ((-skew, skew),) + tuple(
+        (sum(lengths[:g]), lengths[g]) for g in range(n_groups)
+    )
     t_rows, d_rows = tokens // n_tp, tokens // n_dp
     dma = pltpu.SemaphoreType.DMA
     out = pl.pallas_call(
-        functools.partial(kernel, n_rep, n_dp, n_tp, n_k, n_late, n_f, groups),
+        functools.partial(kernel, n_rep, n_dp, n_tp, n_k, n_late, n_skew, n_f, groups),
         out_shape=(
             jax.ShapeDtypeStruct((1, t_rows, cols), bf16),
             jax.ShapeDtypeStruct((1, d_rows, ffn), bf16),
@@ -445,7 +468,7 @@
             jax.ShapeDtypeStruct((ffn, cols), bf16),
             jax.ShapeDtypeStruct((share, cols), bf16),
         ) + tuple(jax.ShapeDtypeStruct((size, cols), bf16) for _, size in groups)
-        + (jax.ShapeDtypeStruct((chunk, cols), bf16),) * (n_x - 1),
+        + (jax.ShapeDtypeStruct((skew, cols), bf16),) * (n_x - 1),
         in_specs=[pl.BlockSpec(memory_space=pl.ANY)] * 5,
         out_specs=[pl.BlockSpec(memory_space=pl.ANY)] * (4 + len(groups) + n_x),
         scratch_shapes=[
@@ -489,8 +512,8 @@
     layer_out, hidden_grad, new_momentum, outer_step = out[:4]
     late, edge = out[5:5 + len(groups)], out[5 + len(groups):]
 
-    def across(value, d):
-        hops = [(2 * x + c, 2 * ((x - d) % n_x) + c) for x in range(n_x) for c in range(2)]
+    def across(value, d, cores=(0, 1)):
+        hops = [(2 * x + c, 2 * ((x - d) % n_x) + c) for x in range(n_x) for c in cores]
         return lax.ppermute(value, "rep", hops)
 
     def beside(value):
@@ -498,10 +521,10 @@
         return lax.ppermute(value, "rep", hops)
 
     arrived = []
-    for value in late:
-        arrived.append([across(value, d) for d in range(1, n_x)])
-    near = [beside(value) for value in late]
-    edge_near = [beside(value) for value in edge]
+    for g, value in enumerate(late):
+        cores = (1,) if g == 0 else (0, 1)
+        arrived.append([across(value, d, cores) for d in range(1, n_x)])
+    near = [beside(value) for value in late[1:]]
     results = (layer_out, hidden_grad, new_momentum, outer_step)
     steps = max(
         k for k in range(1, 9)
@@ -526,10 +549,7 @@
     )(*results)
     firsts = [share - late_rows + start for start, _ in groups]
     parts = []
-    for d in range(1, n_x):
-        parts.append((edge[d - 1], share - late_rows - chunk, n_x - d, False))
-        parts.append((edge_near[d - 1], share - late_rows - chunk, n_x - d, True))
-    for first, value, own in zip(firsts, late, near):
+    for first, value, own in zip(firsts[1:], late[1:], near):
         parts += [(value, first, 0, False), (own, first, 0, True)]
     outer_step = place(n_rep, share, outer_step, parts)
 
@@ -541,8 +561,11 @@
             outer_step = lax.dynamic_update_slice(outer_step, value, (owner * share + first, 0))
         return outer_step
 
-    for first, here in zip(firsts, arrived):
+    on_edge = lax.rem(lax.axis_index("rep"), 2) == 0
+    for g, (first, here) in enumerate(zip(firsts, arrived)):
         here, outer_step = lax.optimization_barrier((here, outer_step))
+        if g == 0:
+            here = [jnp.where(on_edge, edge[n_x - 2 - d], value) for d, value in enumerate(here)]
         across_near = [beside(value) for value in here]
         outer_step = put(outer_step, here, first, False)
         outer_step = put(outer_step, across_near, first, True)

time: 350 us -> 367 us (1.049)
  waiting for transfers between devices: 20 us -> 47.6 us
  Pallas kernels: 313 us -> 300 us
    ppermute x4 -> x5, waiting for transfers between devices: 18.9 us -> 43.2 us  [across(): return lax.ppermute(value, 'rep', hops)]
    pallas_call x1, Pallas kernels: 280 us -> 266 us  [per_device(): pl.pallas_call(functools.partial(kernel, n_rep, n_dp, n_tp, n_k, n_late,...]
    dynamic_update_slice x8 -> x9, local copies, waits for them, and re-layouts: 7.92 us -> 9.27 us  [put(): lax.dynamic_update_slice(outer_step, value, (owner * share + first, 0))]
  transfers between devices with their start and end apart: 13 -> 14, of which waited for: 5 -> 9; matrix products, arithmetic and copies ran while one was open for 2% -> 3% of each run, Pallas kernels for 10% -> 9%
where the time goes in v2:
time: 367 us; the launch traced here: 365 us
  Pallas kernels  300 us (82%)
  waiting for transfers between devices  47.6 us (13%)
  local copies, waits for them, and re-layouts  9.27 us (3%)
  starting transfers between devices  4.92 us (1%)
    pallas_call x1, Pallas kernels, per_device(): pl.pallas_call(functools.partial(kernel, n_rep, n_dp, n_tp, n_k, n_late,...  266 us
    ppermute x5, waiting for transfers between devices, across(): return lax.ppermute(value, 'rep', hops)  43.2 us
    pallas_call x1, Pallas kernels, per_device(): pl.pallas_call(copy_bands, out_shape=tuple((jax.ShapeDtypeStruct(r.shape,...  30.1 us
    dynamic_update_slice x9, local copies, waits for them, and re-layouts, put(): lax.dynamic_update_slice(outer_step, value, (owner * share + first, 0))  9.27 us
  transfers between devices with their start and end apart: 14, of which 9 were waited for; matrix products, arithmetic and copies ran while one was open for 3% of the time, Pallas kernels for 9%

profile of v2, /device:TPU:0, one launch (start us, length us, event | category | flops | bytes accessed | tf_op | source)
XLA Modules:
  0.0 365.4 jit_solution(15796920280003070697)
XLA Ops:
  0.6 266.5 %layer_step.1 = (bf16[1,256,2048]{2,1,0:T(8,128)(2,1)}, bf16[1,128,7168]{2,1,0:T(8,128)(2,1)}, f32[1792,2048]{1,0:T(8,128)}, bf16[7168,2048]{1,0:T(8,128)(2,1)},...) custom-call(bf16[1,512,7168]{2,1,0:T(8,128)(2,1)} %hidden.1, ...), custom_call_target="tpu_custom_call" | custom-call | tf_op jit(solution)/shard_map/layer_step/pallas_call | solution.py:462
  267.1 1.7 collective-permute-start.4
  268.8 0.0 collective-permute-start.5
  268.8 0.5 collective-permute-start.6
  269.3 0.5 collective-permute-start.8
  269.8 30.1 %shard_map.84 = (bf16[1,256,2048]{2,1,0:T(8,128)(2,1)}, bf16[1,128,7168]{2,1,0:T(8,128)(2,1)}, f32[1792,2048]{1,0:T(8,128)}, bf16[7168,2048]{1,0:T(8,128)(2,1)}) custom-call(bf16[1,256,2048]{2,1,0:T(8,128)(2,1)} %get-tuple-element.28.refs_0_, bf16[1,128,7168]{2,1,0:T(8,128)(2,1)} %get-tuple-element.29.refs_1_, f32[1792,2048]{1,0:T(8,128)} %get-tuple-element.30.refs_2_, ...), custom_call_target="tpu_custom_call" | custom-call | flops 46923776000 | bytes 93847552 | tf_op jit(solution)/shard_map/pallas_call | solution.py:538
  299.9 0.0 collective-permute-done.8.refs_7_
  299.9 0.6 collective-permute-start.3
  300.5 0.0 collective-permute-done.7.refs_5_
  300.5 3.7 %place.1 = bf16[7168,2048]{1,0:T(8,128)(2,1)} custom-call(bf16[7168,2048]{1,0:T(8,128)(2,1)} %get-tuple-element.40.step, bf16[352,2048]{1,0:T(8,128)(2,1)} %get-tuple-element.38.refs_0_, bf16[352,2048]{1,0:T(8,128)(2,1)} %collective-permute-done.5.refs_1_, bf16[128,2048]{1,0:T(8,128)(2,1)} %get-tuple-element.37.refs_2_, ...), custom_call_target="tpu_custom_call", output_to_operand_aliasing={{}: (0, {})} | custom-call | flops 4718592000 | bytes 9437184 | tf_op jit(solution)/shard_map/place/pallas_call | solution.py:421
  304.2 2.7 constant_dynamic-update-slice_fusion.9
  306.9 2.7 collective-permute-done.9
  309.6 1.0 constant_dynamic-update-slice_fusion.8
  310.6 23.2 %collective-permute-done.3 = bf16[352,2048]{1,0:T(8,128)(2,1)} collective-permute-done((bf16[352,2048]{1,0:T(8,128)(2,1)}, bf16[352,2048]{1,0:T(8,128)(2,1)}, u32[]{:S(2)}, u32[]{:S(2)}) %collective-permute-start.3) | collective-permute-done | bytes 1441824 | tf_op jit(solution)/shard_map/ppermute | solution.py:517
  333.8 0.5 collective-permute-start.2
  334.3 2.6 constant_dynamic-update-slice_fusion.7
  336.9 0.3 collective-permute-done.10
  337.2 1.2 constant_dynamic-update-slice_fusion.6
  338.4 9.9 %collective-permute-done.2 = bf16[128,2048]{1,0:T(8,128)(2,1)S(1)} collective-permute-done((bf16[128,2048]{1,0:T(8,128)(2,1)}, bf16[128,2048]{1,0:T(8,128)(2,1)S(1)}, u32[]{:S(2)}, u32[]{:S(2)}) %collective-permute-start.2) | collective-permute-done | bytes 524320 | tf_op jit(solution)/shard_map/ppermute | solution.py:517
  348.3 0.5 collective-permute-start.1
  348.9 0.8 constant_dynamic-update-slice_fusion.5
  349.7 0.5 collective-permute-done.11
  350.2 0.8 constant_dynamic-update-slice_fusion.4
  351.1 6.2 %collective-permute-done.1 = bf16[64,2048]{1,0:T(8,128)(2,1)S(1)} collective-permute-done((bf16[64,2048]{1,0:T(8,128)(2,1)}, bf16[64,2048]{1,0:T(8,128)(2,1)S(1)}, u32[]{:S(2)}, u32[]{:S(2)}) %collective-permute-start.1) | collective-permute-done | bytes 262176 | tf_op jit(solution)/shard_map/ppermute | solution.py:517
  357.3 0.5 collective-permute-start
  357.8 0.7 constant_dynamic-update-slice_fusion.3
  358.5 0.3 collective-permute-done.12
  358.8 0.7 constant_dynamic-update-slice_fusion.2
  359.5 3.9 %collective-permute-done = bf16[32,2048]{1,0:T(8,128)(2,1)S(1)} collective-permute-done((bf16[32,2048]{1,0:T(8,128)(2,1)}, bf16[32,2048]{1,0:T(8,128)(2,1)S(1)}, u32[]{:S(2)}, u32[]{:S(2)}) %collective-permute-start) | collective-permute-done | bytes 131104 | tf_op jit(solution)/shard_map/ppermute | solution.py:517
  363.4 0.7 constant_dynamic-update-slice_fusion.1
  364.1 0.7 collective-permute-done.13
  364.7 0.7 constant_dynamic-update-slice_fusion
  (9 shorter events, 0.0 us)
Async XLA Ops:
  267.1 37.1 %collective-permute-start.4 = (bf16[256,2048]{1,0:T(8,128)(2,1)}, bf16[256,2048]{1,0:T(8,128)(2,1)}, u32[]{:S(2)}, u32[]{:S(2)}) collective-permute-start(bf16[256,2048]{1,0:T(8,128)(2,1)} %get-tuple-element.39), channel_id=1, source_target_pairs={{8,24},{24,8},{9,25},{25,9},{10,26},{26,10},{11,27},{27,11},{12,28... | collective-permute-start | bytes 3145736 | tf_op jit(solution)/shard_map/ppermute | solution.py:517
  268.8 31.7 %collective-permute-start.5 = (bf16[352,2048]{1,0:T(8,128)(2,1)}, bf16[352,2048]{1,0:T(8,128)(2,1)}, u32[]{:S(2)}, u32[]{:S(2)}) collective-permute-start(bf16[352,2048]{1,0:T(8,128)(2,1)} %get-tuple-element.38.refs_0_), channel_id=1, source_target_pairs={{0,8},{8,0},{16,24},{24,16},{1,9},{9,1},{17,25},{25,17},{2,10},{10... | collective-permute-start | bytes 4325384 | tf_op jit(solution)/shard_map/ppermute | solution.py:521
  268.8 31.7 %collective-permute-start.6 = (bf16[128,2048]{1,0:T(8,128)(2,1)}, bf16[128,2048]{1,0:T(8,128)(2,1)}, u32[]{:S(2)}, u32[]{:S(2)}) collective-permute-start(bf16[128,2048]{1,0:T(8,128)(2,1)} %get-tuple-element.37.refs_2_), channel_id=1, source_target_pairs={{0,8},{8,0},{16,24},{24,16},{1,9},{9,1},{17,25},{25,17},{2,10},{10... | collective-permute-start | bytes 1572872 | tf_op jit(solution)/shard_map/ppermute | solution.py:521
  269.3 31.2 %collective-permute-start.7 = (bf16[64,2048]{1,0:T(8,128)(2,1)}, bf16[64,2048]{1,0:T(8,128)(2,1)}, u32[]{:S(2)}, u32[]{:S(2)}) collective-permute-start(bf16[64,2048]{1,0:T(8,128)(2,1)} %get-tuple-element.36.refs_4_), channel_id=1, source_target_pairs={{0,8},{8,0},{16,24},{24,16},{1,9},{9,1},{17,25},{25,17},{2,10},{10... | collective-permute-start | bytes 786440 | tf_op jit(solution)/shard_map/ppermute | solution.py:521
  269.3 30.6 %collective-permute-start.8 = (bf16[32,2048]{1,0:T(8,128)(2,1)}, bf16[32,2048]{1,0:T(8,128)(2,1)}, u32[]{:S(2)}, u32[]{:S(2)}) collective-permute-start(bf16[32,2048]{1,0:T(8,128)(2,1)} %get-tuple-element.35.refs_6_), channel_id=1, source_target_pairs={{0,8},{8,0},{16,24},{24,16},{1,9},{9,1},{17,25},{25,17},{2,10},{10... | collective-permute-start | bytes 393224 | tf_op jit(solution)/shard_map/ppermute | solution.py:521
  299.9 33.9 %collective-permute-start.3 = (bf16[352,2048]{1,0:T(8,128)(2,1)}, bf16[352,2048]{1,0:T(8,128)(2,1)}, u32[]{:S(2)}, u32[]{:S(2)}) collective-permute-start(bf16[352,2048]{1,0:T(8,128)(2,1)} %get-tuple-element.38.refs_0_), channel_id=1, source_target_pairs={{0,16},{8,24},{16,0},{24,8},{1,17},{9,25},{17,1},{25,9},{2,18},{10... | collective-permute-start | bytes 4325384 | tf_op jit(solution)/shard_map/ppermute | solution.py:517
  306.9 2.7 collective-permute-start.9
  333.8 3.4 collective-permute-start.10
  333.8 14.5 %collective-permute-start.2 = (bf16[128,2048]{1,0:T(8,128)(2,1)}, bf16[128,2048]{1,0:T(8,128)(2,1)S(1)}, u32[]{:S(2)}, u32[]{:S(2)}) collective-permute-start(bf16[128,2048]{1,0:T(8,128)(2,1)} %get-tuple-element.37.refs_2_), channel_id=1, source_target_pairs={{0,16},{8,24},{16,0},{24,8},{1,17},{9,25},{17,1},{25,9},{2,18},{10... | collective-permute-start | bytes 1572872 | tf_op jit(solution)/shard_map/ppermute | solution.py:517
  348.3 1.9 collective-permute-start.11
  348.3 8.9 %collective-permute-start.1 = (bf16[64,2048]{1,0:T(8,128)(2,1)}, bf16[64,2048]{1,0:T(8,128)(2,1)S(1)}, u32[]{:S(2)}, u32[]{:S(2)}) collective-permute-start(bf16[64,2048]{1,0:T(8,128)(2,1)} %get-tuple-element.36.refs_4_), channel_id=1, source_target_pairs={{0,16},{8,24},{16,0},{24,8},{1,17},{9,25},{17,1},{25,9},{2,18},{10... | collective-permute-start | bytes 786440 | tf_op jit(solution)/shard_map/ppermute | solution.py:517
  357.3 1.5 collective-permute-start.12
  357.3 6.1 %collective-permute-start = (bf16[32,2048]{1,0:T(8,128)(2,1)}, bf16[32,2048]{1,0:T(8,128)(2,1)S(1)}, u32[]{:S(2)}, u32[]{:S(2)}) collective-permute-start(bf16[32,2048]{1,0:T(8,128)(2,1)} %get-tuple-element.35.refs_6_), channel_id=1, source_target_pairs={{0,16},{8,24},{16,0},{24,8},{1,17},{9,25},{17,1},{25,9},{2,18},{10... | collective-permute-start | bytes 393224 | tf_op jit(solution)/shard_map/ppermute | solution.py:517
  363.4 1.3 collective-permute-start.13
